TPU v7x, 32 devices: a whole 2x2x4 slice. The times are simulated.
32 devices in a mesh: rep: 2 (over y), ada: 4 (over z), tp: 4 (over x, core).
Axes of the slice: x: 2, y: 2, z: 4, core: 2. Of those that a mesh axis runs over, the one named last changes fastest.
Arguments:
- hidden: bfloat16 [256, 8192], P(('rep', 'ada')), parts along dimension 0, may hold values from -6 to 6
- input_norm_gain: bfloat16 [8192], replicated, may hold values from 0.5 to 1.5
- request_adapter: int32 [256], P(('rep', 'ada')), parts along dimension 0, may hold values from 0 to 15, as said below
- cache_fill_length: int32 [256], P(('rep', 'ada')), parts along dimension 0, may hold values from 1 to 512, as said below
- query_weight: bfloat16 [8192, 8192], P('ada', 'tp'), may hold values from -0.0625 to 0.0625
- key_weight: bfloat16 [8192, 1024], P('ada', 'tp'), may hold values from -0.0625 to 0.0625
- value_weight: bfloat16 [8192, 1024], P('ada', 'tp'), may hold values from -0.0625 to 0.0625
- output_weight: bfloat16 [8192, 8192], P('tp', 'ada'), may hold values from -0.0625 to 0.0625
- down_weight_all: bfloat16 [8192, 512], P('tp', 'ada'), may hold values from -0.0625 to 0.0625
- query_up_weight: bfloat16 [256, 8192], P('ada', 'tp'), may hold values from -1.5 to 1.5
- value_up_weight: bfloat16 [256, 1024], P('ada', 'tp'), may hold values from -1.5 to 1.5
- rotated_key_cache: bfloat16 [256, 512, 1024], P(('rep', 'ada'), None, 'tp'), parts along dimension 0, may hold values from -768 to 768
- stored_value_cache: bfloat16 [256, 512, 1024], P(('rep', 'ada'), None, 'tp'), parts along dimension 0, may hold values from -6 to 6
Outputs:
- layer_out: bfloat16 [256, 8192], P(('rep', 'tp'), 'ada'), parts along dimension 0
- new_key: bfloat16 [256, 1024], P(('rep', 'ada'), 'tp'), parts along dimension 0
- new_value: bfloat16 [256, 1024], P(('rep', 'ada'), 'tp'), parts along dimension 0
There are 2 independent parts, one for each index of `rep`. A program takes and returns all parts, laid end to end along the dimension named above; an argument that names none is the same for every part. Nothing has to cross between parts.
Inputs may be any that keep to these rules, and one draw needn't show every extreme that they name: `request_adapter`: among the 32 requests of one ada index (aligned blocks), at most 16 name adapters of one group 4 * o to 4 * o + 3; in every draw one group is named by exactly 16 requests of every block. `cache_fill_length`: within each part of rep the 128 lengths sum to 32768, and some request of each part has exactly 512.
All inputs are finite; a program needn't handle non-finite values.
Results may differ from a plain program's by a relative error of at most 0.012.
The roundings to bfloat16 on the way count: a program that leaves them out, or rounds other values in their place, can miss the bound.
Values may be sent and summed in bfloat16 or wider, within the bound.
No kernel may reach another device: no remote copies, remote signals or barrier semaphores. Data moves between devices by JAX's collectives and lax.ppermute only.
A program may use at most 64 MiB of HBM per device.

v0:
```python
import jax
import jax.numpy as jnp
from jax import lax
from jax.sharding import PartitionSpec as P

QUERY_HEAD_COUNT = 64
KEY_VALUE_HEADS = 8
HEAD_WIDTH = 128
ADAPTER_RANK = 16
ADAPTER_SCALE = 2.0
EPSILON = 1e-05
ROPE_BASE = 500000.0


def rotary(vectors, positions):
    count_rows = vectors.shape[0]
    split_heads = vectors.reshape(count_rows, -1, HEAD_WIDTH)
    halfway = HEAD_WIDTH // 2
    frequency = ROPE_BASE ** (-2.0 * jnp.arange(halfway, dtype=jnp.float32) / HEAD_WIDTH)
    angles = positions.astype(jnp.float32)[:, None] * frequency[None, :]
    cosine = jnp.cos(angles)[:, None, :]
    sine_part = jnp.sin(angles)[:, None, :]
    leading = split_heads[..., :halfway]
    trailing = split_heads[..., halfway:]
    turned = jnp.concatenate(
        [leading * cosine - trailing * sine_part, trailing * cosine + leading * sine_part], axis=-1
    )
    return turned.reshape(count_rows, -1)


def on_device(
    hidden,
    input_norm_gain,
    request_adapter,
    cache_fill_length,
    query_weight,
    key_weight,
    value_weight,
    output_weight,
    down_weight_all,
    query_up_weight,
    value_up_weight,
    rotated_key_cache,
    stored_value_cache,
):
    req_local = hidden.shape[0]
    owners = lax.axis_size("ada")
    tp_index = lax.axis_index("tp")
    portion_width = down_weight_all.shape[0]
    grouped_by_holder = down_weight_all.shape[1] // (2 * ADAPTER_RANK)
    capacity = max(2, (2 * req_local + owners - 1) // owners)
    slot_total = owners * capacity
    q_width = query_weight.shape[1]
    kv_width = key_weight.shape[1]
    widened = hidden.astype(jnp.float32)
    inverse = lax.rsqrt(jnp.mean(widened * widened, axis=-1, keepdims=True) + EPSILON)
    normalized_input = (widened * inverse * input_norm_gain.astype(jnp.float32)[None, :]).astype(
        jnp.bfloat16
    )
    normed_cols, hidden_cols = (
        lax.all_to_all(normalized_input, "ada", split_axis=1, concat_axis=0, tiled=True),
        lax.all_to_all(hidden, "ada", split_axis=1, concat_axis=0, tiled=True),
    )
    owner_of = request_adapter // grouped_by_holder
    sub_of = request_adapter % grouped_by_holder
    row_ids = jnp.arange(req_local, dtype=jnp.int32)
    same_owner = owner_of[:, None] == owner_of[None, :]
    earlier = row_ids[:, None] > row_ids[None, :]
    slot_of = jnp.sum(jnp.logical_and(same_owner, earlier), axis=1)
    target = owner_of * capacity + slot_of
    picker = jnp.arange(slot_total, dtype=jnp.int32)[:, None] == target[None, :]
    my_slice = lax.dynamic_slice_in_dim(
        normalized_input, tp_index * portion_width, portion_width, 1
    )
    send_rows = jnp.dot(
        picker.astype(jnp.bfloat16), my_slice, preferred_element_type=jnp.float32
    ).astype(jnp.bfloat16)
    send_rows = send_rows.reshape(owners, capacity, portion_width)
    row_meta = jnp.stack([sub_of, row_ids], axis=1).astype(jnp.float32)
    send_meta = jnp.dot(
        picker.astype(jnp.float32), row_meta, precision=lax.Precision.HIGHEST
    ).astype(jnp.bfloat16)
    send_meta = send_meta.reshape(owners, capacity, 2)
    rows_in = lax.all_to_all(send_rows, "ada", split_axis=0, concat_axis=0, tiled=True)
    meta_in = lax.all_to_all(send_meta, "ada", split_axis=0, concat_axis=0, tiled=True)
    sources = rows_in.shape[0]
    item_count = rows_in.shape[1]
    flattened_rows = rows_in.reshape(sources * item_count, portion_width)
    value_partial = jnp.dot(flattened_rows, down_weight_all, preferred_element_type=jnp.float32)
    down_projected = lax.psum(value_partial, "tp")
    sub_in = meta_in[..., 0].astype(jnp.int32).reshape(-1)
    column_owner = jnp.arange(value_partial.shape[1], dtype=jnp.int32) // (2 * ADAPTER_RANK)
    chosen = jnp.where(column_owner[None, :] == sub_in[:, None], down_projected, 0.0).astype(
        jnp.bfloat16
    )
    split_rank = chosen.reshape(-1, grouped_by_holder, 2 * ADAPTER_RANK)
    query_down_part = split_rank[:, :, :ADAPTER_RANK].reshape(-1, grouped_by_holder * ADAPTER_RANK)
    value_down_part = split_rank[:, :, ADAPTER_RANK:].reshape(-1, grouped_by_holder * ADAPTER_RANK)
    adapter_update = ADAPTER_SCALE * jnp.concatenate(
        [
            jnp.dot(query_down_part, query_up_weight, preferred_element_type=jnp.float32),
            jnp.dot(value_down_part, value_up_weight, preferred_element_type=jnp.float32),
        ],
        axis=1,
    )
    row_global = jnp.arange(sources, dtype=jnp.int32)[:, None] * req_local + meta_in[..., 1].astype(
        jnp.int32
    )
    adapter_update, row_global = (adapter_update.reshape(sources, item_count, -1), row_global)
    flat_correction = adapter_update.reshape(-1, adapter_update.shape[2])
    flat_target = row_global.reshape(-1)
    term_rows = jnp.concatenate(
        [
            jnp.dot(normed_cols, query_weight, preferred_element_type=jnp.float32),
            jnp.dot(normed_cols, key_weight, preferred_element_type=jnp.float32),
            jnp.dot(normed_cols, value_weight, preferred_element_type=jnp.float32),
        ],
        axis=1,
    )
    picker_in = (
        jnp.arange(req_local * lax.axis_size("ada"), dtype=jnp.int32)[:, None]
        == flat_target[None, :]
    ).astype(jnp.float32)
    placed_in = jnp.dot(picker_in, flat_correction, precision=lax.Precision.HIGHEST)
    filler = jnp.zeros((req_local * lax.axis_size("ada"), kv_width), jnp.float32)
    summed_qkv = lax.psum_scatter(
        term_rows
        + jnp.concatenate([placed_in[:, :q_width], filler, placed_in[:, q_width:]], axis=1),
        "ada",
        scatter_dimension=0,
        tiled=True,
    )
    query_matrix_rows = summed_qkv[:, :q_width]
    key_rows = summed_qkv[:, q_width : q_width + kv_width]
    value_matrix_rows = summed_qkv[:, q_width + kv_width :]
    rotated_query = rotary(query_matrix_rows, cache_fill_length).astype(jnp.bfloat16)
    new_key = rotary(key_rows, cache_fill_length).astype(jnp.bfloat16)
    new_value = value_matrix_rows.astype(jnp.bfloat16)
    kv_local = kv_width // HEAD_WIDTH
    groups = QUERY_HEAD_COUNT // KEY_VALUE_HEADS
    context_len = rotated_key_cache.shape[1]
    score_scale = HEAD_WIDTH ** (-0.5)
    query_heads = rotated_query.reshape(req_local, kv_local, groups, HEAD_WIDTH)
    key_heads = rotated_key_cache.reshape(req_local, context_len, kv_local, HEAD_WIDTH)
    value_heads = stored_value_cache.reshape(req_local, context_len, kv_local, HEAD_WIDTH)
    scores = (
        jnp.einsum("rkgd,rckd->rkgc", query_heads, key_heads, preferred_element_type=jnp.float32)
        * score_scale
    )
    own_score = (
        jnp.einsum(
            "rkgd,rkd->rkg",
            query_heads,
            new_key.reshape(req_local, kv_local, HEAD_WIDTH),
            preferred_element_type=jnp.float32,
        )
        * score_scale
    )
    in_cache = jnp.arange(context_len, dtype=jnp.int32)[None, :] < cache_fill_length[:, None]
    in_cache = in_cache[:, None, None, :]
    masked = jnp.where(in_cache, scores, -1e30)
    row_max = jnp.maximum(jnp.max(masked, axis=-1), own_score)
    exp_terms = jnp.where(in_cache, jnp.exp(masked - row_max[..., None]), 0.0)
    own_exp = jnp.exp(own_score - row_max)
    denominator = jnp.sum(exp_terms, axis=-1) + own_exp
    weights_low = (exp_terms / denominator[..., None]).astype(jnp.bfloat16)
    own_low = (own_exp / denominator).astype(jnp.bfloat16)
    mixed_heads = jnp.einsum(
        "rkgc,rckd->rkgd", weights_low, value_heads, preferred_element_type=jnp.float32
    )
    mixed_heads = mixed_heads + own_low.astype(jnp.float32)[..., None] * new_value.reshape(
        req_local, kv_local, 1, HEAD_WIDTH
    ).astype(jnp.float32)
    context = mixed_heads.reshape(req_local, -1).astype(jnp.bfloat16)
    partial_out = jnp.dot(
        lax.all_gather(context, "ada", axis=0, tiled=True),
        output_weight,
        preferred_element_type=jnp.float32,
    )
    summed = lax.psum_scatter(partial_out, "tp", scatter_dimension=0, tiled=True)
    share_rows = summed.shape[0]
    residual = lax.dynamic_slice_in_dim(hidden_cols, tp_index * share_rows, share_rows, 0).astype(
        jnp.float32
    )
    layer_out = (residual + summed).astype(jnp.bfloat16)
    return (layer_out, new_key, new_value)


def solution(mesh):
    return jax.shard_map(
        on_device,
        mesh=mesh,
        in_specs=(
            P(("rep", "ada"), None),
            P(),
            P(("rep", "ada")),
            P(("rep", "ada")),
            P("ada", "tp"),
            P("ada", "tp"),
            P("ada", "tp"),
            P("tp", "ada"),
            P("tp", "ada"),
            P("ada", "tp"),
            P("ada", "tp"),
            P(("rep", "ada"), None, "tp"),
            P(("rep", "ada"), None, "tp"),
        ),
        out_specs=(P(("rep", "tp"), "ada"), P(("rep", "ada"), "tp"), P(("rep", "ada"), "tp")),
        check_vma=False,
    )
```

profile of v0, /device:TPU:0, one launch (start us, length us, event | category | flops | bytes accessed | tf_op | source)
XLA Modules:
  0.0 159.5 jit_solution(8979767625529145039)
XLA Ops:
  9.0 6.3 %all-to-all-start.2 = ((bf16[4,16,2]{1,2,0:T(2,128)(2,1)}), bf16[4,16,2]{1,2,0:T(2,128)(2,1)S(1)}, u32[]{:S(2)}, u32[]{:S(2)}) async-start(bf16[4,16,2]{1,2,0:T(2,128)(2,1)} %copy.51), calls=%async_computation.2 | async-start | bytes 4096 | tf_op jit(solution)/shard_map/all_to_all | solution.py:85
  16.0 1.2 fusion.18
  17.3 1.2 fusion.20
  18.5 0.9 convolution_convert_fusion
  19.4 1.4 all-to-all-done.2
  20.8 3.7 %all-to-all-start.3 = ((bf16[4,16,2048]{2,1,0:T(8,128)(2,1)}), bf16[4,16,2048]{2,1,0:T(8,128)(2,1)S(1)}, u32[]{:S(2)}, u32[]{:S(2)}) async-start(bf16[4,16,2048]{2,1,0:T(8,128)(2,1)} %bitcast.6), calls=%async_computation.3 | async-start | bytes 524288 | tf_op jit(solution)/shard_map/all_to_all | solution.py:84
  25.7 7.1 %all-to-all-done.3 = bf16[4,16,2048]{2,1,0:T(8,128)(2,1)S(1)} async-done(((bf16[4,16,2048]{2,1,0:T(8,128)(2,1)}), bf16[4,16,2048]{2,1,0:T(8,128)(2,1)S(1)}, u32[]{:S(2)}, u32[]{:S(2)}) %all-to-all-start.3) | async-done | bytes 262176 | tf_op jit(solution)/shard_map/all_to_all | solution.py:84
  32.9 3.5 %all-to-all-start.1 = ((bf16[32,4,2048]{2,0,1:T(8,128)(2,1)}), bf16[32,4,2048]{2,0,1:T(8,128)(2,1)S(1)}, u32[]{:S(2)}, u32[]{:S(2)}) async-start(bf16[32,4,2048]{2,0,1:T(8,128)(2,1)} %bitcast.93), calls=%async_computation.1 | async-start | bytes 1048576 | tf_op jit(solution)/shard_map/all_to_all | solution.py:61
  36.4 1.3 fusion.57
  37.6 10.6 %psum.7 = bf16[64,128]{1,0:T(8,128)(2,1)S(1)} all-reduce(f32[64,128]{1,0:T(8,128)S(1)} %fusion.57), channel_id=1, replica_groups=mesh['rep'=2,'ada'=4,'tp'=4] {'tp'}, use_global_device_ids=true, to_apply=%region_2.3 | all-reduce | flops 8192 | bytes 49152 | tf_op jit(solution)/shard_map/psum | solution.py:90
  48.4 0.9 fusion.59
  49.4 1.2 fusion.58
  51.4 4.7 %fusion.54 = f32[128,2048]{1,0:T(8,128)S(1)} fusion(bf16[128,2048]{1,0:T(8,128)(2,1)S(1)} %bitcast.97, bf16[2048,2048]{1,0:T(8,128)(2,1)} %param.17), kind=kOutput, calls=%fused_computation.94 | convolution fusion | flops 1073741824 | bytes 9961472 | tf_op jit(solution)/shard_map/dot_general | solution.py:114
  56.8 1.3 maximum_add_fusion
  58.4 32.9 %reduce-scatter.3.cloned.1.call-done = f32[32,2560]{1,0:T(8,128)} async-done(((f32[128,2560]{1,0:T(8,128)}), f32[32,2560]{1,0:T(8,128)}) %reduce-scatter.3.cloned.1.call-update) | async-done | bytes 327696 | tf_op jit(solution)/shard_map/reduce_scatter | solution.py:126
  92.0 1.0 slice_bitcast_fusion
  93.8 5.8 %fusion.53 = (f32[32,2,8]{2,1,0:T(2,128)S(1)}, f32[32,2,8,512]{3,2,1,0:T(8,128)S(1)}) fusion(bf16[32,16,64]{2,1,0:T(8,128)(2,1)S(1)} %get-tuple-element.6, bf16[32,16,64]{2,1,0:T(8,128)(2,1)S(1)} %get-tuple-element.5, pred[32,512]{1,0:T(8,128)(4,1)S(1)} %iota_compare_fusion.1, bf16[32,512,256]{2,1,0:T(8,128)(2,1)} %param.24), kind=kOutput, calls=%fused_computation.93 | convolution fusion | flops 68156928 | bytes 9586688 | tf_op jit(solution)/shard_map/rkgd,rckd->rkgc/dot_general | solution.py:147
  101.3 4.7 %fusion.15 = bf16[32,2,8,128]{3,2,1,0:T(8,128)(2,1)S(1)} fusion(f32[32,2,8,512]{3,2,1,0:T(8,128)S(1)} %get-tuple-element.18, f32[32,2,8]{2,1,0:T(2,128)S(1)} %copy.57, f32[32,2,8]{2,1,0:T(2,128)S(1)} %copy.55, pred[32,512]{1,0:T(8,128)(4,1)S(1)} %iota_compare_fusion.1, f32[32,2,128]{2,1,0:T(2,128)S(1)} %reshape.194, f32[32,2,8]{2,1,0:T(2,128)S(1)} %copy.59, ...), kind=kOutput, calls=%fused_computation.13 | convolution fusion | flops 68354048 | bytes 9623552 | tf_op jit(solution)/shard_map/rkgc,rckd->rkgd/dot_general | solution.py:168
  106.0 16.0 %all_gather.3 = bf16[128,2048]{1,0:T(8,128)(2,1)S(1)} all-gather(bf16[32,2048]{1,0:T(8,128)(2,1)S(1)} %bitcast.105), channel_id=1, replica_groups=mesh['rep'=2,'ada'=4,'tp'=4] {'ada'}, dimensions={0}, use_global_device_ids=true | all-gather | bytes 655360 | tf_op jit(solution)/shard_map/all_gather | solution.py:176
  122.0 5.7 %fusion.60 = f32[128,2048]{1,0:T(8,128)} fusion(bf16[128,2048]{1,0:T(8,128)(2,1)S(1)} %all_gather.3, bf16[2048,2048]{1,0:T(8,128)(2,1)} %param.20), kind=kOutput, calls=%fused_computation.100 | convolution fusion | flops 1073741824 | bytes 9961472 | tf_op jit(solution)/shard_map/dot_general | solution.py:175
  128.6 3.5 %all-to-all-start = ((bf16[32,4,2048]{2,0,1:T(8,128)(2,1)}), bf16[32,4,2048]{2,0,1:T(8,128)(2,1)S(1)}, u32[]{:S(2)}, u32[]{:S(2)}) async-start(bf16[32,4,2048]{2,0,1:T(8,128)(2,1)} %bitcast.94), calls=%async_computation | async-start | bytes 1048576 | tf_op jit(solution)/shard_map/all_to_all | solution.py:62
  132.8 10.1 %all-to-all-done = bf16[32,4,2048]{2,0,1:T(8,128)(2,1)S(1)} async-done(((bf16[32,4,2048]{2,0,1:T(8,128)(2,1)}), bf16[32,4,2048]{2,0,1:T(8,128)(2,1)S(1)}, u32[]{:S(2)}, u32[]{:S(2)}) %all-to-all-start) | async-done | bytes 524320 | tf_op jit(solution)/shard_map/all_to_all | solution.py:62
  142.9 8.1 %reduce-scatter.5.cloned.1.call-done = f32[32,2048]{1,0:T(8,128)} async-done(((f32[128,2048]{1,0:T(8,128)}), f32[32,2048]{1,0:T(8,128)}) %reduce-scatter.5.cloned.1.call-update) | async-done | bytes 262160 | tf_op jit(solution)/shard_map/reduce_scatter | solution.py:180
  151.0 1.6 %add_convert_fusion = bf16[32,2048]{1,0:T(8,128)(2,1)} fusion(f32[32,2048]{1,0:T(8,128)} %reduce-scatter.5.cloned.1.call-done, bf16[128,2048]{1,0:T(8,128)(2,1)S(1)} %bitcast.104, s32[]{:T(128)S(6)} %select_n.38), kind=kLoop, calls=%fused_computation.33 | loop fusion | flops 196608 | bytes 524292 | tf_op jit(solution)/shard_map/convert_element_type | solution.py:185
  (69 shorter events, 10.4 us)
Async XLA Ops:
  7.2 48.9 %copy-start = (bf16[2048,256]{1,0:T(8,128)(2,1)S(1)}, bf16[2048,256]{1,0:T(8,128)(2,1)}, u32[]{:S(2)}) copy-start(bf16[2048,256]{1,0:T(8,128)(2,1)} %param.18) | copy-start | bytes 3145732
  9.0 11.8 %all-to-all-start.2 = ((bf16[4,16,2]{1,2,0:T(2,128)(2,1)}), bf16[4,16,2]{1,2,0:T(2,128)(2,1)S(1)}, u32[]{:S(2)}, u32[]{:S(2)}) async-start(bf16[4,16,2]{1,2,0:T(2,128)(2,1)} %copy.51), calls=%async_computation.2 | async-start | bytes 4096 | tf_op jit(solution)/shard_map/all_to_all | solution.py:85
  20.8 12.0 %all-to-all-start.3 = ((bf16[4,16,2048]{2,1,0:T(8,128)(2,1)}), bf16[4,16,2048]{2,1,0:T(8,128)(2,1)S(1)}, u32[]{:S(2)}, u32[]{:S(2)}) async-start(bf16[4,16,2048]{2,1,0:T(8,128)(2,1)} %bitcast.6), calls=%async_computation.3 | async-start | bytes 524288 | tf_op jit(solution)/shard_map/all_to_all | solution.py:84
  32.9 18.5 %all-to-all-start.1 = ((bf16[32,4,2048]{2,0,1:T(8,128)(2,1)}), bf16[32,4,2048]{2,0,1:T(8,128)(2,1)S(1)}, u32[]{:S(2)}, u32[]{:S(2)}) async-start(bf16[32,4,2048]{2,0,1:T(8,128)(2,1)} %bitcast.93), calls=%async_computation.1 | async-start | bytes 1048576 | tf_op jit(solution)/shard_map/all_to_all | solution.py:61
  36.3 54.9 %reduce-scatter.3.cloned.1.call-start = ((), (), s32[]{:S(2)}) async-start(), calls=%async_computation.6 | async-start | bytes 1638400 | tf_op jit(solution)/shard_map/reduce_scatter | solution.py:126
  51.3 5.1 %copy-start.2 = (bf16[2048,256]{1,0:T(8,128)(2,1)S(1)}, bf16[2048,256]{1,0:T(8,128)(2,1)}, u32[]{:S(2)}) copy-start(bf16[2048,256]{1,0:T(8,128)(2,1)} %param.19) | copy-start | bytes 3145732
  51.3 6.8 %copy-start.4 = (s32[32]{0:T(128)S(1)}, s32[32]{0:T(128)}, u32[]{:S(2)}) copy-start(s32[32]{0:T(128)} %param.16) | copy-start | bytes 388
  58.1 93.0 %reduce-scatter.5.cloned.1.call-start = ((), (), s32[]{:S(2)}) async-start(), calls=%async_computation.7 | async-start | bytes 1310720 | tf_op jit(solution)/shard_map/reduce_scatter | solution.py:180
  101.2 26.4 %copy-start.3 = (bf16[32,256]{1,0:T(8,128)(2,1)}, bf16[32,256]{1,0:T(8,128)(2,1)S(1)}, u32[]{:S(2)}) copy-start(bf16[32,256]{1,0:T(8,128)(2,1)S(1)} %slice.82) | copy-start | bytes 49156
  122.0 5.8 %copy-start.1 = (bf16[32,8192]{1,0:T(8,128)(2,1)S(1)}, bf16[32,8192]{1,0:T(8,128)(2,1)}, u32[]{:S(2)}) copy-start(bf16[32,8192]{1,0:T(8,128)(2,1)} %param.13) | copy-start | bytes 1572868
  128.6 14.3 %all-to-all-start = ((bf16[32,4,2048]{2,0,1:T(8,128)(2,1)}), bf16[32,4,2048]{2,0,1:T(8,128)(2,1)S(1)}, u32[]{:S(2)}, u32[]{:S(2)}) async-start(bf16[32,4,2048]{2,0,1:T(8,128)(2,1)} %bitcast.94), calls=%async_computation | async-start | bytes 1048576 | tf_op jit(solution)/shard_map/all_to_all | solution.py:62
Sparse Core Ops, SparseCore 0:
  58.2 33.0 reduce-scatter.2
  127.8 23.1 reduce-scatter.4
where the time goes:
time: 160 us; the launch traced here: 159 us
  waiting for transfers between devices  59.6 us (37%)
  matrix products  26.9 us (17%)
  blocking collectives  26.5 us (17%)
  starting transfers between devices  17.1 us (11%)
  between operations  14.3 us (9%)
  other arithmetic  8.31 us (5%)
  local copies, waits for them, and re-layouts  6.7 us (4%)
    reduce_scatter x1, waiting for transfers between devices, on_device(): lax.psum_scatter(term_rows + jnp.concatenate([placed_in[:, :q_width], fil...  32.9 us
    all_gather x1, blocking collectives, on_device(): lax.all_gather(context, 'ada', axis=0, tiled=True)  16 us
    psum x1, blocking collectives, on_device(): down_projected = lax.psum(value_partial, 'tp')  10.6 us
    all_to_all x1, waiting for transfers between devices, on_device(): lax.all_to_all(hidden, 'ada', split_axis=1, concat_axis=0, tiled=True)  10.1 us
    reduce_scatter x1, waiting for transfers between devices, on_device(): lax.psum_scatter(partial_out, 'tp', scatter_dimension=0, tiled=True)  8.12 us
    all_to_all x1, waiting for transfers between devices, on_device(): lax.all_to_all(send_rows, 'ada', split_axis=0, concat_axis=0, tiled=True)  7.11 us
    all_to_all x1, starting transfers between devices, on_device(): lax.all_to_all(send_meta, 'ada', split_axis=0, concat_axis=0, tiled=True)  6.35 us
    dot_general x1, matrix products, on_device(): jnp.einsum('rkgd,rckd->rkgc', query_heads, key_heads, preferred_element_t...  5.81 us
  transfers between devices with their start and end apart: 6, of which 5 were waited for; matrix products, arithmetic and copies ran while one was open for 7% of the time, Pallas kernels for 0%

commit v1 on v0

--- a/solution.py
+++ b/solution.py
@@ -2,6 +2,7 @@
 import jax.numpy as jnp
 from jax import lax
 from jax.sharding import PartitionSpec as P
+from jax.lax import axis_size, ppermute
 
 QUERY_HEAD_COUNT = 64
 KEY_VALUE_HEADS = 8
@@ -10,6 +11,14 @@
 ADAPTER_SCALE = 2.0
 EPSILON = 1e-05
 ROPE_BASE = 500000.0
+
+
+def things_answer(inner_x):
+    spare = inner_x
+    shares = axis_size("tp")
+    for i0 in [[(k0, k0 ^ d) for k0 in range(shares)] for d in (1, 2, 4, 8, 16) if d < shares]:
+        spare = spare + ppermute(spare, "tp", i0)
+    return spare
 
 
 def rotary(vectors, positions):
@@ -87,7 +96,7 @@
     item_count = rows_in.shape[1]
     flattened_rows = rows_in.reshape(sources * item_count, portion_width)
     value_partial = jnp.dot(flattened_rows, down_weight_all, preferred_element_type=jnp.float32)
-    down_projected = lax.psum(value_partial, "tp")
+    down_projected = things_answer(value_partial)
     sub_in = meta_in[..., 0].astype(jnp.int32).reshape(-1)
     column_owner = jnp.arange(value_partial.shape[1], dtype=jnp.int32) // (2 * ADAPTER_RANK)
     chosen = jnp.where(column_owner[None, :] == sub_in[:, None], down_projected, 0.0).astype(

time: 160 us -> 160 us (level)
  blocking collectives: 26.5 us -> 15.9 us
  waiting for transfers between devices: 59.6 us -> 68.8 us
    all_to_all x1, waiting for transfers between devices: 0.01 us -> 11.4 us  [on_device(): lax.all_to_all(normalized_input, 'ada', split_axis=1, concat_axis=0, tile...]
    psum x1 -> x0, blocking collectives: 10.6 us -> none  [on_device(): down_projected = lax.psum(value_partial, 'tp')]
    reduce_scatter x1, waiting for transfers between devices: 32.9 us -> 29.4 us  [on_device(): lax.psum_scatter(term_rows + jnp.concatenate([placed_in[:, :q_width], fil...]
    all_to_all x1, starting transfers between devices: 6.35 us -> 3.22 us  [on_device(): lax.all_to_all(send_meta, 'ada', split_axis=0, concat_axis=0, tiled=True)]
    all_to_all x1, starting transfers between devices: 3.74 us -> 6.35 us  [on_device(): lax.all_to_all(send_rows, 'ada', split_axis=0, concat_axis=0, tiled=True)]
  transfers between devices with their start and end apart: 6 -> 8, of which waited for: 5 -> 7; matrix products, arithmetic and copies ran while one was open for 7% -> 5% of each run, Pallas kernels for 0% -> 0%
where the time goes in v1:
time: 160 us; the launch traced here: 159 us
  waiting for transfers between devices  68.8 us (43%)
  matrix products  26.9 us (17%)
  starting transfers between devices  18.3 us (11%)
  blocking collectives  15.9 us (10%)
  between operations  14.3 us (9%)
  other arithmetic  8.31 us (5%)
  local copies, waits for them, and re-layouts  6.69 us (4%)
    reduce_scatter x1, waiting for transfers between devices, on_device(): lax.psum_scatter(term_rows + jnp.concatenate([placed_in[:, :q_width], fil...  29.4 us
    all_gather x1, blocking collectives, on_device(): lax.all_gather(context, 'ada', axis=0, tiled=True)  15.9 us
    all_to_all x1, waiting for transfers between devices, on_device(): lax.all_to_all(normalized_input, 'ada', split_axis=1, concat_axis=0, tile...  11.4 us
    all_to_all x1, waiting for transfers between devices, on_device(): lax.all_to_all(hidden, 'ada', split_axis=1, concat_axis=0, tiled=True)  10.1 us
    reduce_scatter x1, waiting for transfers between devices, on_device(): lax.psum_scatter(partial_out, 'tp', scatter_dimension=0, tiled=True)  8.09 us
    all_to_all x1, waiting for transfers between devices, on_device(): lax.all_to_all(send_rows, 'ada', split_axis=0, concat_axis=0, tiled=True)  8.07 us
    all_to_all x1, starting transfers between devices, on_device(): lax.all_to_all(send_rows, 'ada', split_axis=0, concat_axis=0, tiled=True)  6.35 us
    dot_general x1, matrix products, on_device(): jnp.einsum('rkgd,rckd->rkgc', query_heads, key_heads, preferred_element_t...  5.81 us
  transfers between devices with their start and end apart: 8, of which 7 were waited for; matrix products, arithmetic and copies ran while one was open for 5% of the time, Pallas kernels for 0%

profile of v1, /device:TPU:0, one launch (start us, length us, event | category | flops | bytes accessed | tf_op | source)
XLA Modules:
  0.0 159.1 jit_solution(14084791862385536307)
XLA Ops:
  8.9 1.2 fusion.18
  10.1 1.2 fusion.20
  12.3 6.3 %all-to-all-start.3 = ((bf16[4,16,2048]{2,1,0:T(8,128)(2,1)}), bf16[4,16,2048]{2,1,0:T(8,128)(2,1)S(1)}, u32[]{:S(2)}, u32[]{:S(2)}) async-start(bf16[4,16,2048]{2,1,0:T(8,128)(2,1)} %bitcast.6), calls=%async_computation.3 | async-start | bytes 524288 | tf_op jit(solution)/shard_map/all_to_all | solution.py:93
  19.5 8.1 %all-to-all-done.3 = bf16[4,16,2048]{2,1,0:T(8,128)(2,1)S(1)} async-done(((bf16[4,16,2048]{2,1,0:T(8,128)(2,1)}), bf16[4,16,2048]{2,1,0:T(8,128)(2,1)S(1)}, u32[]{:S(2)}, u32[]{:S(2)}) %all-to-all-start.3) | async-done | bytes 262176 | tf_op jit(solution)/shard_map/all_to_all | solution.py:93
  27.5 3.2 %all-to-all-start.2 = ((bf16[4,16,2]{1,2,0:T(2,128)(2,1)}), bf16[4,16,2]{1,2,0:T(2,128)(2,1)S(1)}, u32[]{:S(2)}, u32[]{:S(2)}) async-start(bf16[4,16,2]{1,2,0:T(2,128)(2,1)} %copy.51), calls=%async_computation.2 | async-start | bytes 4096 | tf_op jit(solution)/shard_map/all_to_all | solution.py:94
  30.8 1.3 fusion.57
  33.3 1.5 collective-permute-start.1
  34.8 1.4 all-to-all-done.2
  36.2 3.6 %all-to-all-start.1 = ((bf16[32,4,2048]{2,0,1:T(8,128)(2,1)}), bf16[32,4,2048]{2,0,1:T(8,128)(2,1)S(1)}, u32[]{:S(2)}, u32[]{:S(2)}) async-start(bf16[32,4,2048]{2,0,1:T(8,128)(2,1)} %bitcast.93), calls=%async_computation.1 | async-start | bytes 1048576 | tf_op jit(solution)/shard_map/all_to_all | solution.py:70
  40.3 0.9 fusion.59
  41.2 1.2 fusion.58
  43.2 11.4 %all-to-all-done.1 = bf16[32,4,2048]{2,0,1:T(8,128)(2,1)S(1)} async-done(((bf16[32,4,2048]{2,0,1:T(8,128)(2,1)}), bf16[32,4,2048]{2,0,1:T(8,128)(2,1)S(1)}, u32[]{:S(2)}, u32[]{:S(2)}) %all-to-all-start.1) | async-done | bytes 524320 | tf_op jit(solution)/shard_map/all_to_all | solution.py:70
  54.6 4.7 %fusion.54 = f32[128,2048]{1,0:T(8,128)S(1)} fusion(bf16[128,2048]{1,0:T(8,128)(2,1)S(1)} %bitcast.97, bf16[2048,2048]{1,0:T(8,128)(2,1)} %param.17), kind=kOutput, calls=%fused_computation.94 | convolution fusion | flops 1073741824 | bytes 9961472 | tf_op jit(solution)/shard_map/dot_general | solution.py:123
  60.0 1.3 maximum_add_fusion
  61.6 29.4 %reduce-scatter.3.cloned.1.call-done = f32[32,2560]{1,0:T(8,128)} async-done(((f32[128,2560]{1,0:T(8,128)}), f32[32,2560]{1,0:T(8,128)}) %reduce-scatter.3.cloned.1.call-update) | async-done | bytes 327696 | tf_op jit(solution)/shard_map/reduce_scatter | solution.py:135
  91.8 1.0 slice_bitcast_fusion
  93.6 5.8 %fusion.53 = (f32[32,2,8]{2,1,0:T(2,128)S(1)}, f32[32,2,8,512]{3,2,1,0:T(8,128)S(1)}) fusion(bf16[32,16,64]{2,1,0:T(8,128)(2,1)S(1)} %get-tuple-element.6, bf16[32,16,64]{2,1,0:T(8,128)(2,1)S(1)} %get-tuple-element.5, pred[32,512]{1,0:T(8,128)(4,1)S(1)} %iota_compare_fusion.1, bf16[32,512,256]{2,1,0:T(8,128)(2,1)} %param.24), kind=kOutput, calls=%fused_computation.93 | convolution fusion | flops 68156928 | bytes 9586688 | tf_op jit(solution)/shard_map/rkgd,rckd->rkgc/dot_general | solution.py:156
  101.0 4.7 %fusion.15 = bf16[32,2,8,128]{3,2,1,0:T(8,128)(2,1)S(1)} fusion(f32[32,2,8,512]{3,2,1,0:T(8,128)S(1)} %get-tuple-element.18, f32[32,2,8]{2,1,0:T(2,128)S(1)} %copy.57, f32[32,2,8]{2,1,0:T(2,128)S(1)} %copy.55, pred[32,512]{1,0:T(8,128)(4,1)S(1)} %iota_compare_fusion.1, f32[32,2,128]{2,1,0:T(2,128)S(1)} %reshape.194, f32[32,2,8]{2,1,0:T(2,128)S(1)} %copy.59, ...), kind=kOutput, calls=%fused_computation.13 | convolution fusion | flops 68354048 | bytes 9623552 | tf_op jit(solution)/shard_map/rkgc,rckd->rkgd/dot_general | solution.py:177
  105.8 15.9 %all_gather.3 = bf16[128,2048]{1,0:T(8,128)(2,1)S(1)} all-gather(bf16[32,2048]{1,0:T(8,128)(2,1)S(1)} %bitcast.105), channel_id=1, replica_groups=mesh['rep'=2,'ada'=4,'tp'=4] {'ada'}, dimensions={0}, use_global_device_ids=true | all-gather | bytes 655360 | tf_op jit(solution)/shard_map/all_gather | solution.py:185
  121.7 5.7 %fusion.60 = f32[128,2048]{1,0:T(8,128)} fusion(bf16[128,2048]{1,0:T(8,128)(2,1)S(1)} %all_gather.3, bf16[2048,2048]{1,0:T(8,128)(2,1)} %param.20), kind=kOutput, calls=%fused_computation.100 | convolution fusion | flops 1073741824 | bytes 9961472 | tf_op jit(solution)/shard_map/dot_general | solution.py:184
  128.3 3.5 %all-to-all-start = ((bf16[32,4,2048]{2,0,1:T(8,128)(2,1)}), bf16[32,4,2048]{2,0,1:T(8,128)(2,1)S(1)}, u32[]{:S(2)}, u32[]{:S(2)}) async-start(bf16[32,4,2048]{2,0,1:T(8,128)(2,1)} %bitcast.94), calls=%async_computation | async-start | bytes 1048576 | tf_op jit(solution)/shard_map/all_to_all | solution.py:71
  132.5 10.1 %all-to-all-done = bf16[32,4,2048]{2,0,1:T(8,128)(2,1)S(1)} async-done(((bf16[32,4,2048]{2,0,1:T(8,128)(2,1)}), bf16[32,4,2048]{2,0,1:T(8,128)(2,1)S(1)}, u32[]{:S(2)}, u32[]{:S(2)}) %all-to-all-start) | async-done | bytes 524320 | tf_op jit(solution)/shard_map/all_to_all | solution.py:71
  142.6 8.1 %reduce-scatter.5.cloned.1.call-done = f32[32,2048]{1,0:T(8,128)} async-done(((f32[128,2048]{1,0:T(8,128)}), f32[32,2048]{1,0:T(8,128)}) %reduce-scatter.5.cloned.1.call-update) | async-done | bytes 262160 | tf_op jit(solution)/shard_map/reduce_scatter | solution.py:189
  150.7 1.6 %add_convert_fusion = bf16[32,2048]{1,0:T(8,128)(2,1)} fusion(f32[32,2048]{1,0:T(8,128)} %reduce-scatter.5.cloned.1.call-done, bf16[128,2048]{1,0:T(8,128)(2,1)S(1)} %bitcast.104, s32[]{:T(128)S(6)} %select_n.38), kind=kLoop, calls=%fused_computation.33 | loop fusion | flops 196608 | bytes 524292 | tf_op jit(solution)/shard_map/convert_element_type | solution.py:194
  (73 shorter events, 11.5 us)
Async XLA Ops:
  7.2 52.2 %copy-start = (bf16[2048,256]{1,0:T(8,128)(2,1)S(1)}, bf16[2048,256]{1,0:T(8,128)(2,1)}, u32[]{:S(2)}) copy-start(bf16[2048,256]{1,0:T(8,128)(2,1)} %param.18) | copy-start | bytes 3145732
  12.3 15.3 %all-to-all-start.3 = ((bf16[4,16,2048]{2,1,0:T(8,128)(2,1)}), bf16[4,16,2048]{2,1,0:T(8,128)(2,1)S(1)}, u32[]{:S(2)}, u32[]{:S(2)}) async-start(bf16[4,16,2048]{2,1,0:T(8,128)(2,1)} %bitcast.6), calls=%async_computation.3 | async-start | bytes 524288 | tf_op jit(solution)/shard_map/all_to_all | solution.py:93
  27.5 8.7 %all-to-all-start.2 = ((bf16[4,16,2]{1,2,0:T(2,128)(2,1)}), bf16[4,16,2]{1,2,0:T(2,128)(2,1)S(1)}, u32[]{:S(2)}, u32[]{:S(2)}) async-start(bf16[4,16,2]{1,2,0:T(2,128)(2,1)} %copy.51), calls=%async_computation.2 | async-start | bytes 4096 | tf_op jit(solution)/shard_map/all_to_all | solution.py:94
  32.0 1.3 collective-permute-start
  33.3 6.8 %collective-permute-start.1 = (f32[64,128]{1,0:T(8,128)S(1)}, f32[64,128]{1,0:T(8,128)S(1)}, u32[]{:S(2)}, u32[]{:S(2)}) collective-permute-start(f32[64,128]{1,0:T(8,128)S(1)} %add.83), channel_id=1, source_target_pairs={{0,2},{1,3},{2,0},{3,1},{4,6},{5,7},{6,4},{7,5},{8,10},{9,11},{10,... | collective-permute-start | bytes 98312 | tf_op jit(solution)/shard_map/ppermute | solution.py:20
  36.2 18.4 %all-to-all-start.1 = ((bf16[32,4,2048]{2,0,1:T(8,128)(2,1)}), bf16[32,4,2048]{2,0,1:T(8,128)(2,1)S(1)}, u32[]{:S(2)}, u32[]{:S(2)}) async-start(bf16[32,4,2048]{2,0,1:T(8,128)(2,1)} %bitcast.93), calls=%async_computation.1 | async-start | bytes 1048576 | tf_op jit(solution)/shard_map/all_to_all | solution.py:70
  39.9 51.1 %reduce-scatter.3.cloned.1.call-start = ((), (), s32[]{:S(2)}) async-start(), calls=%async_computation.6 | async-start | bytes 1638400 | tf_op jit(solution)/shard_map/reduce_scatter | solution.py:135
  54.6 5.1 %copy-start.2 = (bf16[2048,256]{1,0:T(8,128)(2,1)S(1)}, bf16[2048,256]{1,0:T(8,128)(2,1)}, u32[]{:S(2)}) copy-start(bf16[2048,256]{1,0:T(8,128)(2,1)} %param.19) | copy-start | bytes 3145732
  54.6 6.7 %copy-start.4 = (s32[32]{0:T(128)S(1)}, s32[32]{0:T(128)}, u32[]{:S(2)}) copy-start(s32[32]{0:T(128)} %param.16) | copy-start | bytes 388
  61.3 89.4 %reduce-scatter.5.cloned.1.call-start = ((), (), s32[]{:S(2)}) async-start(), calls=%async_computation.7 | async-start | bytes 1310720 | tf_op jit(solution)/shard_map/reduce_scatter | solution.py:189
  101.0 26.4 %copy-start.3 = (bf16[32,256]{1,0:T(8,128)(2,1)}, bf16[32,256]{1,0:T(8,128)(2,1)S(1)}, u32[]{:S(2)}) copy-start(bf16[32,256]{1,0:T(8,128)(2,1)S(1)} %slice.82) | copy-start | bytes 49156
  121.7 5.7 %copy-start.1 = (bf16[32,8192]{1,0:T(8,128)(2,1)S(1)}, bf16[32,8192]{1,0:T(8,128)(2,1)}, u32[]{:S(2)}) copy-start(bf16[32,8192]{1,0:T(8,128)(2,1)} %param.13) | copy-start | bytes 1572868
  128.3 14.3 %all-to-all-start = ((bf16[32,4,2048]{2,0,1:T(8,128)(2,1)}), bf16[32,4,2048]{2,0,1:T(8,128)(2,1)S(1)}, u32[]{:S(2)}, u32[]{:S(2)}) async-start(bf16[32,4,2048]{2,0,1:T(8,128)(2,1)} %bitcast.94), calls=%async_computation | async-start | bytes 1048576 | tf_op jit(solution)/shard_map/all_to_all | solution.py:71
Sparse Core Ops, SparseCore 0:
  61.4 29.5 reduce-scatter.2
  127.5 23.0 reduce-scatter.4
